TPU v7x, 128 devices: a whole 4x4x4 slice. The times are simulated.
128 devices in a mesh: pair: 16 (over x, z_lo, core), ga: 8 (over z_hi, y).
Axes of the slice: x: 4, y: 4, z: 4 (z_hi: 2, z_lo: 2; z = z_hi * 2 + z_lo), core: 2. Of those that a mesh axis runs over, the one named last changes fastest.
Arguments:
- densities: bfloat16 [24576, 4096], P('pair', 'ga'), may hold values from -6 to 6
- val_band: int32 [24576], P('pair'), may hold values from 0 to 127
- cond_band: int32 [24576], P('pair'), may hold values from 0 to 255
- val_energy: float32 [128], replicated, may hold values from -12 to -1
- cond_energy: float32 [256], replicated, may hold values from 1 to 12
Outputs:
- chi: float32 [4096, 4096], P('ga', 'pair')
All inputs are finite; a program needn't handle non-finite values.
Results may differ from a plain program's by a relative error of at most 0.0012.
Values may be sent and summed in bfloat16 or wider, within the bound.
A program may use at most 128 MiB of HBM per device.

v0:
```python
import math

import jax
import jax.numpy as jnp
from jax import lax
from jax.sharding import PartitionSpec as P


def lookup(bands, table):
    levels = lax.broadcasted_iota(jnp.int32, (1, table.shape[0]), 1)
    onehot = (bands[:, None] == levels).astype(jnp.float32)
    return jnp.sum(onehot * table[None, :], axis=1)


def per_device(densities, val_band, cond_band, val_energy, cond_energy):
    pairs_total = densities.shape[0] * lax.axis_size("pair")
    gap = lookup(val_band, val_energy) - lookup(cond_band, cond_energy)
    weight = 4.0 / (gap * math.sqrt(pairs_total))
    scaled = (weight[:, None] * densities.astype(jnp.float32)).astype(jnp.bfloat16)
    gathered = lax.all_gather(densities, "ga", axis=1, tiled=True)
    owned = lax.psum_scatter(
        lax.dot_general(
            gathered, scaled, (((0,), (0,)), ((), ())), preferred_element_type=jnp.float32
        ),
        "pair",
        scatter_dimension=0,
        tiled=True,
    )
    return owned.T


def solution(mesh):
    placed = (P("pair", "ga"), P("pair"), P("pair"), P(), P())
    return jax.shard_map(
        per_device, mesh=mesh, in_specs=placed, out_specs=P("ga", "pair"), check_vma=False
    )
```

profile of v0, /device:TPU:67, one launch (start us, length us, event | category | flops | bytes accessed | tf_op | source)
XLA Modules:
  0.0 286.9 jit_solution(14027633360789709186)
XLA Ops:
  6.5 0.0 copy-start
  6.5 0.0 copy-start.3
  6.5 0.0 copy-start.2
  6.5 0.0 copy-start.1
  6.5 0.0 all-gather.2.cloned.1.call-start
  6.6 0.7 all-gather.2.cloned.1.call-update
  7.3 0.0 reduce-scatter.2.cloned.1.call-start
  7.3 0.0 copy-done.3
  7.3 1.2 select_reduce_fusion.1
  8.5 0.0 copy-done.2
  8.5 0.0 copy-done.1
  8.5 0.5 select_reduce_fusion
  9.1 160.4 %all-gather.2.cloned.1.call-done = bf16[1536,4096]{1,0:T(8,128)(2,1)} async-done(((bf16[1536,512]{1,0:T(8,128)(2,1)}), bf16[1536,4096]{1,0:T(8,128)(2,1)}) %all-gather.2.cloned.1.call-update) | async-done | bytes 12582928 | tf_op jit(solution)/shard_map/all_gather | solution.py:20
  169.4 0.0 copy-done
  169.4 12.0 %convolution_bitcast_fusion = f32[4096,512]{0,1:T(8,128)} fusion(bf16[1536,4096]{1,0:T(8,128)(2,1)} %all-gather.2.cloned.1.call-done, bf16[1536,512]{1,0:T(8,128)(2,1)S(1)} %copy-done, f32[1536]{0:T(1024)S(1)} %multiply_divide_fusion), kind=kOutput, calls=%fused_computation | convolution fusion | flops 6444810240 | bytes 22550528 | tf_op jit(solution)/shard_map/dot_general | solution.py:22
  181.4 0.0 reduce-scatter.2.cloned.1.call-update
  181.5 98.6 %reduce-scatter.2.cloned.1.call-done = f32[256,512]{0,1:T(8,128)} async-done(((f32[4096,512]{0,1:T(8,128)}), f32[256,512]{0,1:T(8,128)}) %reduce-scatter.2.cloned.1.call-update) | async-done | bytes 524304 | tf_op jit(solution)/shard_map/reduce_scatter | solution.py:21
  (1 shorter events, 0.0 us)
Async XLA Ops:
  6.5 162.9 %copy-start = (bf16[1536,512]{1,0:T(8,128)(2,1)S(1)}, bf16[1536,512]{1,0:T(8,128)(2,1)}, u32[]{:S(2)}) copy-start(bf16[1536,512]{1,0:T(8,128)(2,1)} %param.5) | copy-start | bytes 4718596
  6.5 0.8 copy-start.3
  6.5 2.0 copy-start.2
  6.5 2.0 copy-start.1
  6.5 162.9 %all-gather.2.cloned.1.call-start = ((), (), s32[]{:S(2)}) async-start(), calls=%async_computation.1 | async-start | bytes 14155776 | tf_op jit(solution)/shard_map/all_gather | solution.py:20
  7.3 272.8 %reduce-scatter.2.cloned.1.call-start = ((), (), s32[]{:S(2)}) async-start(), calls=%async_computation.2 | async-start | bytes 8912896 | tf_op jit(solution)/shard_map/reduce_scatter | solution.py:21
Sparse Core Ops, SparseCore 0:
  9.5 159.8 all-gather.1
  181.6 98.4 reduce-scatter.1
where the time goes:
time: 290 us; the launch traced here: 287 us
  waiting for transfers between devices  260 us (90%)
  between operations  13.4 us (5%)
  matrix products  12 us (4%)
    all_gather x1, waiting for transfers between devices, per_device(): gathered = lax.all_gather(densities, 'ga', axis=1, tiled=True)  160 us
    reduce_scatter x1, waiting for transfers between devices, per_device(): lax.psum_scatter(lax.dot_general(gathered, scaled, (((0,), (0,)), ((), ()...  98.6 us
    dot_general x1, matrix products, per_device(): lax.dot_general(gathered, scaled, (((0,), (0,)), ((), ())), preferred_ele...  12 us
  transfers between devices with their start and end apart: 2, of which 2 were waited for; matrix products, arithmetic and copies ran while one was open for 1% of the time, Pallas kernels for 0%

commit v1 on v0

v1 whole, which is shorter than its diff:
```python
import math

import jax
import jax.numpy as jnp
from jax import lax
from jax.experimental import pallas as pl
from jax.experimental.pallas import tpu as pltpu
from jax.sharding import PartitionSpec as P

MESH = pl.DeviceIdType.MESH
F32 = jnp.float32
BF16 = jnp.bfloat16
NB = 6


def kernel(
    pairs_total,
    dens, vb, cb, ve, ce,
    out,
    own, y1b, y2b, trb, pb, lo, lp, wt,
    pp, cr, xs0, xr0, xs, xr, xo, tl, lr, fs, fm, db, mb,
    own_sem, y1_s, y1_r, p_s, p_r, tr_s, tr_r, y2_s, y2_r,
    c_s, c_r, x_s, x_r, l_s, l_r, fd_s, fm_s, d_r, m_r,
):
    pair = lax.axis_index("pair")
    g = lax.axis_index("ga")
    x, l, c = pair // 4, (pair // 2) % 2, pair % 2
    h, y = g // 4, g % 4
    kh = y // 2
    y_up, y_dn, y_far = (y + 1) % 4, (y + 3) % 4, (y + 2) % 4

    def remote(src, dst, ss, rs, dev):
        return pltpu.make_async_remote_copy(
            src_ref=src, dst_ref=dst, send_sem=ss, recv_sem=rs, device_id=dev, device_id_type=MESH
        )

    def load_copy(j):
        return pltpu.make_async_copy(
            dens.at[:, :, pl.ds(j * 128, 128)], own.at[j], own_sem.at[j]
        )

    def y1_copy(j):
        return remote(own.at[j], y1b.at[j], y1_s.at[j], y1_r.at[j], (pair, h * 4 + y_dn))

    def p_copy(j):
        return remote(own.at[j], pb.at[j], p_s.at[j], p_r.at[j], (pair, (1 - h) * 4 + y))

    def tr_copy(j):
        return remote(own.at[j, 1 - kh], trb.at[j], tr_s.at[j], tr_r.at[j], (pair, h * 4 + y_up))

    def y2_copy(j):
        return remote(trb.at[j], y2b.at[j], y2_s.at[j], y2_r.at[j], (pair, h * 4 + y_up))

    def core_copy(w, j):
        return remote(
            pp.at[w, j], cr.at[w, j // 2], c_s.at[w, j // 2], c_r.at[w, j // 2],
            (x * 4 + l * 2 + 1 - c, g),
        )

    def x_copy(w, jl, d):
        to = (x + d) % 4
        dev = (to * 4 + l * 2 + c, g)
        if isinstance(w, int) and w == 0:
            return remote(xs0.at[jl, to], xr0.at[jl, d - 1], x_s.at[0, jl, d - 1], x_r.at[0, jl, d - 1], dev)
        return remote(xs.at[w - 1, jl, to], xr.at[w - 1, jl, d - 1], x_s.at[w, jl, d - 1], x_r.at[w, jl, d - 1], dev)

    def l_copy(w):
        return remote(tl.at[w, 1 - l], lr.at[w], l_s.at[w], l_r.at[w], (x * 4 + (1 - l) * 2 + c, g))

    def rows_cols(w):
        p_g = (1 - h) * 4 + y
        row = p_g if w >= 4 else g
        col = {0: g, 1: h * 4 + y_up, 2: h * 4 + y_far, 3: p_g, 4: h * 4 + y_up, 5: h * 4 + y_far}[w]
        return row, col

    def direct_copy(w):
        row, col = rows_cols(w)
        return remote(fs.at[w], db.at[x, c], fd_s.at[w], d_r.at[x, c], (2 * col + l, row))

    def mirror_copy(w):
        row, col = rows_cols(w)
        return remote(fm.at[w], mb.at[2 * l + c, x % 2], fm_s.at[w], m_r.at[2 * l + c, x % 2], (2 * row + x // 2, col))

    for j in range(4):
        load_copy(j).start()
    for j in range(4):
        load_copy(j).wait()
        y1_copy(j).start()
        p_copy(j).start()
        tr_copy(j).start()

    level = lax.broadcasted_iota(jnp.int32, (128, 128), 0)
    tv = jnp.broadcast_to(ve[...], (128, 128)).T
    tc0 = jnp.broadcast_to(ce[0:1, :], (128, 128)).T
    tc1 = jnp.broadcast_to(ce[1:2, :], (128, 128)).T
    for k in range(12):
        v_row = vb[k:k + 1, :]
        c_row = cb[k:k + 1, :]
        val = jnp.sum(jnp.where(level == v_row, tv, 0.0), axis=0, keepdims=True)
        con = jnp.sum(
            jnp.where(level == c_row, tc0, 0.0) + jnp.where(level + 128 == c_row, tc1, 0.0),
            axis=0, keepdims=True,
        )
        wt[k:k + 1, :] = 4.0 / ((val - con) * math.sqrt(pairs_total))

    def scale_into(src, j, dst):
        for k in range(12):
            tile = src[j, k // 6, (k % 6) * 128:(k % 6) * 128 + 128, :].astype(F32).T
            tile = (tile * wt[k:k + 1, :]).astype(BF16)
            dst[k // 6, pl.ds(pl.multiple_of(j * 128, 128), 128), (k % 6) * 128:(k % 6) * 128 + 128] = tile

    def dot(a, b):
        return lax.dot_general(a, b, (((1,), (0,)), ((), ())), preferred_element_type=F32)

    def csend(w, j):
        @pl.when(c != j % 2)
        def _():
            core_copy(w, j).start()

    def consume(w, j):
        jl = j // 2

        @pl.when(c == j % 2)
        def _():
            core_copy(w, j).wait_recv()
            total = pp[w, j] + cr[w, jl]
            for i in range(4):
                if w == 0:
                    xs0[jl, i] = total[i * 128:(i + 1) * 128]
                else:
                    xs[w - 1, jl, i] = total[i * 128:(i + 1) * 128].astype(BF16)
            mine = pl.ds(pl.multiple_of(x * 128, 128), 128)
            xo[w, jl] = pp[w, j, mine, :] + cr[w, jl, mine, :]
            for d in (2, 1, 3):
                x_copy(w, jl, d).start()

    def x_reduce(w):
        for jl in range(2):
            for d in (1, 2, 3):
                x_copy(w, jl, d).wait_recv()
            if w == 0:
                tl[w, jl] = xo[w, jl] + xr0[jl, 0] + xr0[jl, 1] + xr0[jl, 2]
            else:
                tl[w, jl] = (
                    xo[w, jl] + xr[w - 1, jl, 0].astype(F32)
                    + xr[w - 1, jl, 1].astype(F32) + xr[w - 1, jl, 2].astype(F32)
                )
        l_copy(w).start()

    def deliver(w):
        l_copy(w).wait_recv()
        total = tl[w, l] + lr[w]
        fs[w] = total
        if w >= 1:
            fm[w] = total.T
            mirror_copy(w).start()
        if w >= 4:
            direct_copy(w).start()
        else:
            row, col = rows_cols(w)

            @pl.when(2 * col + l == pair)
            def _():
                db[x, c] = fs[w]

            @pl.when(2 * col + l != pair)
            def _():
                direct_copy(w).start()

    @pl.loop(0, 4)
    def _(j):
        scale_into(own, j, lo)

    @pl.loop(0, 4)
    def _(j):
        pp[0, j] = dot(lo[0], own[j, 0]) + dot(lo[1], own[j, 1])
        csend(0, j)

    @pl.loop(0, 4)
    def _(j):
        consume(0, j)

    @pl.loop(0, 4)
    def _(k):
        y1_copy(k).wait_recv()
        pp[1, k] = dot(lo[0], y1b[k, 0]) + dot(lo[1], y1b[k, 1])
        csend(1, k)

        @pl.when(k < 2)
        def _():
            for t in range(2):
                tr_copy(2 * k + t).wait_recv()
                y2_copy(2 * k + t).start()

        p_copy(k).wait_recv()
        pp[3, k] = dot(lo[h], pb[k, h])
        csend(3, k)
        scale_into(pb, k, lp)
        consume(1, k)
        y2_copy(k).wait_recv()
        pp[2, k] = dot(lo[kh], y2b[k])
        csend(2, k)
        consume(3, k)
        consume(2, k)

    x_reduce(0)

    @pl.loop(0, 4)
    def _(j):
        pp[4, j] = dot(lp[0], y1b[j, 0]) + dot(lp[1], y1b[j, 1])
        csend(4, j)
        pp[5, j] = dot(lp[kh], y2b[j])
        csend(5, j)

    deliver(0)
    x_reduce(1)
    x_reduce(3)

    @pl.loop(0, 4)
    def _(j):
        consume(4, j)
        consume(5, j)

    x_reduce(2)
    deliver(1)
    deliver(3)
    deliver(2)
    x_reduce(4)
    x_reduce(5)
    deliver(4)
    deliver(5)

    col = pair // 2
    dy = (col % 4 - y + 4) % 4
    dh = jnp.where(col // 4 != h, 1, 0)
    has_d = dy <= 2
    has_m = (dy >= 2) | ((dy == 0) & (dh == 1))
    here = (c == l) & ((dh == 0) | (dy == 0)) & has_d

    for i in range(4):
        for cc in range(2):
            @pl.when(has_d & jnp.logical_not(here & (x == i) & (c == cc)))
            def _(i=i, cc=cc):
                remote(fs.at[0], db.at[i, cc], fd_s.at[0], d_r.at[i, cc], (pair, (1 - h) * 4 + y)).wait_recv()

            @pl.when(has_m)
            def _(i=i, cc=cc):
                remote(fm.at[1], mb.at[i, cc], fm_s.at[1], m_r.at[i, cc], (pair, (1 - h) * 4 + y)).wait_recv()

    def emit(pick):
        for i in range(4):
            for cc in range(2):
                out[i * 128:(i + 1) * 128, cc * 128:(cc + 1) * 128] = pick(i, cc)

    @pl.when(has_d & has_m)
    def _():
        emit(lambda i, cc: db[i, cc] + mb[i, cc])

    @pl.when(has_d & jnp.logical_not(has_m))
    def _():
        emit(lambda i, cc: db[i, cc])

    @pl.when(jnp.logical_not(has_d))
    def _():
        emit(lambda i, cc: mb[i, cc])

    @pl.loop(0, 4)
    def _(j):
        y1_copy(j).wait_send()
        p_copy(j).wait_send()
        tr_copy(j).wait_send()
        y2_copy(j).wait_send()
        for w in range(NB):
            @pl.when(c != j % 2)
            def _(w=w):
                core_copy(w, j).wait_send()

    for w in range(NB):
        for jl in range(2):
            for d in (1, 2, 3):
                x_copy(w, jl, d).wait_send()
        l_copy(w).wait_send()
        if w >= 1:
            mirror_copy(w).wait_send()
        if w >= 4:
            direct_copy(w).wait_send()
        else:
            row, col_w = rows_cols(w)

            @pl.when(2 * col_w + l != pair)
            def _(w=w):
                direct_copy(w).wait_send()


def per_device(densities, val_band, cond_band, val_energy, cond_energy):
    pairs, cols = densities.shape
    pairs_total = pairs * lax.axis_size("pair")
    vm = pltpu.VMEM
    dma = pltpu.SemaphoreType.DMA
    scratch = [
        vm((4, 2, 768, 128), BF16), vm((4, 2, 768, 128), BF16), vm((4, 768, 128), BF16),
        vm((4, 768, 128), BF16), vm((4, 2, 768, 128), BF16),
        vm((2, 512, 768), BF16), vm((2, 512, 768), BF16), vm((12, 128), F32),
        vm((NB, 4, 512, 128), F32), vm((NB, 2, 512, 128), F32),
        vm((2, 4, 128, 128), F32), vm((2, 3, 128, 128), F32),
        vm((NB - 1, 2, 4, 128, 128), BF16), vm((NB - 1, 2, 3, 128, 128), BF16),
        vm((NB, 2, 128, 128), F32), vm((NB, 2, 128, 128), F32), vm((NB, 128, 128), F32),
        vm((NB, 128, 128), F32), vm((NB, 128, 128), F32),
        vm((4, 2, 128, 128), F32), vm((4, 2, 128, 128), F32),
        dma((4,)), dma((4,)), dma((4,)), dma((4,)), dma((4,)), dma((4,)), dma((4,)), dma((4,)), dma((4,)),
        dma((NB, 2)), dma((NB, 2)), dma((NB, 2, 3)), dma((NB, 2, 3)), dma((NB,)), dma((NB,)),
        dma((NB,)), dma((NB,)), dma((4, 2)), dma((4, 2)),
    ]
    in_vmem = pl.BlockSpec(memory_space=pltpu.VMEM)

    def body(*refs):
        kernel(pairs_total, *refs)

    return pl.pallas_call(
        body,
        name="chi",
        out_shape=jax.ShapeDtypeStruct((512, 256), F32),
        in_specs=[pl.BlockSpec(memory_space=pl.ANY)] + [in_vmem] * 4,
        out_specs=in_vmem,
        scratch_shapes=scratch,
        compiler_params=pltpu.CompilerParams(
            has_side_effects=True, vmem_limit_bytes=40 * 1024 * 1024
        ),
    )(
        densities.reshape(2, pairs // 2, cols),
        val_band.reshape(12, 128),
        cond_band.reshape(12, 128),
        val_energy.reshape(1, 128),
        cond_energy.reshape(2, 128),
    )


def solution(mesh):
    placed = (P("pair", "ga"), P("pair"), P("pair"), P(), P())
    return jax.shard_map(
        per_device, mesh=mesh, in_specs=placed, out_specs=P("ga", "pair"), check_vma=False
    )
```

time: 290 us -> 93.9 us (0.32)
  waiting for transfers between devices: 260 us -> 0 us
  Pallas kernels: 0 us -> 87.5 us
  between operations: 13.4 us -> 0.01 us
  matrix products: 12 us -> 0 us
  local copies, waits for them, and re-layouts: 0.01 us -> 4.93 us
    all_gather x1 -> x0, waiting for transfers between devices: 160 us -> none  [per_device(): gathered = lax.all_gather(densities, 'ga', axis=1, tiled=True)]
    reduce_scatter x1 -> x0, waiting for transfers between devices: 98.6 us -> none  [per_device(): lax.psum_scatter(lax.dot_general(gathered, scaled, (((0,), (0,)), ((), ()...]
    pallas_call x0 -> x1, Pallas kernels: none -> 87.5 us  [per_device(): pl.pallas_call(body, name='chi', out_shape=jax.ShapeDtypeStruct((512, 256...]
    dot_general x1 -> x0, matrix products: 12 us -> none  [per_device(): lax.dot_general(gathered, scaled, (((0,), (0,)), ((), ())), preferred_ele...]
    unnamed x8 -> x11, local copies, waits for them, and re-layouts: 0.01 us -> 4.93 us
  transfers between devices with their start and end apart: 2 -> 0, of which waited for: 2 -> 0; matrix products, arithmetic and copies ran while one was open for 1% -> 0% of each run, Pallas kernels for 0% -> 0%
where the time goes in v1:
time: 93.9 us; the launch traced here: 92.5 us
  Pallas kernels  87.5 us (93%)
  local copies, waits for them, and re-layouts  4.93 us (5%)
    pallas_call x1, Pallas kernels, per_device(): pl.pallas_call(body, name='chi', out_shape=jax.ShapeDtypeStruct((512, 256...  87.5 us
    unnamed x11, local copies, waits for them, and re-layouts  4.93 us

profile of v1, /device:TPU:67, one launch (start us, length us, event | category | flops | bytes accessed | tf_op | source)
XLA Modules:
  0.0 92.5 jit_solution(12059845064050602560)
XLA Ops:
  0.0 0.0 copy-start
  0.0 1.4 %copy-done = bf16[1536,512]{1,0:T(8,128)(2,1)S(1)} copy-done((bf16[1536,512]{1,0:T(8,128)(2,1)S(1)}, bf16[1536,512]{1,0:T(8,128)(2,1)}, u32[]{:S(2)}) %copy-start) | copy-done | bytes 1572888
  1.4 0.0 copy-start.1
  1.4 0.7 copy-done.1
  2.1 0.0 copy-start.2
  2.1 0.7 copy-done.2
  2.8 0.0 copy-start.3
  2.8 0.7 copy-done.3
  3.5 0.0 copy-start.4
  3.5 0.7 copy-done.4
  4.1 87.5 %chi.1 = f32[512,256]{1,0:T(8,128)S(1)} custom-call(bf16[2,768,512]{2,1,0:T(8,128)(2,1)S(1)} %bitcast.5, s32[12,128]{1,0:T(8,128)S(1)} %bitcast.6, s32[12,128]{1,0:T(8,128)S(1)} %bitcast.7, f32[1,128]{1,0:T(1,128)S(1)} %bitcast.9, f32[2,128]{1,0:T(2,128)S(1)} %bitcast.8), custom_call_target="tpu_custom_call" | custom-call | tf_op jit(solution)/shard_map/chi/pallas_call | solution.py:319
  91.7 0.8 copy.7
Async XLA Ops:
  0.0 1.4 %copy-start = (bf16[1536,512]{1,0:T(8,128)(2,1)S(1)}, bf16[1536,512]{1,0:T(8,128)(2,1)}, u32[]{:S(2)}) copy-start(bf16[1536,512]{1,0:T(8,128)(2,1)} %param.5) | copy-start | bytes 4718596
  1.4 0.7 copy-start.1
  2.1 0.7 copy-start.2
  2.8 0.7 copy-start.3
  3.5 0.7 copy-start.4

commit v2 on v0

v2 whole, which is shorter than its diff:
```python
import math

import jax
import jax.numpy as jnp
from jax import lax
from jax.experimental import pallas as pl
from jax.experimental.pallas import tpu as pltpu
from jax.sharding import PartitionSpec as P

MESH = pl.DeviceIdType.MESH
F32 = jnp.float32
BF16 = jnp.bfloat16
NB = 6


def kernel(
    pairs_total,
    dens, vb_in, cb_in, ve_in, ce_in,
    out,
    own, y1b, y2b, trb, pb, lo, lp, wt, vb, cb, ve, ce,
    pp, cr, xs0, xr0, xs, xr, xo, tl, lr, fs, fm, db, mb,
    in_sem, own_sem, y1_s, y1_r, p_s, p_r, tr_s, tr_r, y2_s, y2_r,
    c_s, c_r, x_s, x_r, l_s, l_r, fd_s, fm_s, d_r, m_r,
):
    pair = lax.axis_index("pair")
    g = lax.axis_index("ga")
    x, l, c = pair // 4, (pair // 2) % 2, pair % 2
    h, y = g // 4, g % 4
    kh = y // 2
    y_up, y_dn, y_far = (y + 1) % 4, (y + 3) % 4, (y + 2) % 4
    other = (1 - h) * 4 + y
    scope = jax.named_scope

    def remote(src, dst, ss, rs, dev):
        return pltpu.make_async_remote_copy(
            src_ref=src, dst_ref=dst, send_sem=ss, recv_sem=rs, device_id=dev, device_id_type=MESH
        )

    def load_copy(j):
        return pltpu.make_async_copy(
            dens.at[:, :, pl.ds(j * 128, 128)], own.at[j], own_sem.at[j]
        )

    def small_copy(i):
        src, dst = ((vb_in, vb), (cb_in, cb), (ve_in, ve), (ce_in, ce))[i]
        return pltpu.make_async_copy(src, dst, in_sem.at[i])

    def y1_copy(j):
        return remote(own.at[j], y1b.at[j], y1_s.at[j], y1_r.at[j], (pair, h * 4 + y_dn))

    def p_copy(j):
        return remote(own.at[j], pb.at[j], p_s.at[j], p_r.at[j], (pair, other))

    def tr_copy(j):
        return remote(own.at[j, 1 - kh], trb.at[j], tr_s.at[j], tr_r.at[j], (pair, h * 4 + y_up))

    def y2_copy(j):
        return remote(trb.at[j], y2b.at[j], y2_s.at[j], y2_r.at[j], (pair, h * 4 + y_up))

    def core_copy(w, j, first, n, part):
        rows = pl.ds(first * 128, n * 128)
        return remote(
            pp.at[w, j, rows], cr.at[w, j // 2, rows], c_s.at[w, j // 2, part], c_r.at[w, j // 2, part],
            (x * 4 + l * 2 + 1 - c, g),
        )

    def x_copy(w, jl, to, slot):
        dev = (to * 4 + l * 2 + c, g)
        if w == 0:
            return remote(xs0.at[jl, to], xr0.at[jl, slot], x_s.at[0, jl, to], x_r.at[0, jl, slot], dev)
        return remote(xs.at[w - 1, jl, to], xr.at[w - 1, jl, slot], x_s.at[w, jl, to], x_r.at[w, jl, slot], dev)

    def l_copy(w):
        return remote(tl.at[w, 1 - l], lr.at[w], l_s.at[w], l_r.at[w], (x * 4 + (1 - l) * 2 + c, g))

    def rows_cols(w):
        row = other if w >= 4 else g
        col = {0: g, 1: h * 4 + y_up, 2: h * 4 + y_far, 3: other, 4: h * 4 + y_up, 5: h * 4 + y_far}[w]
        return row, col

    def stays(w):
        row, col = rows_cols(w)
        return 2 * col + l == pair

    def direct_copy(w):
        row, col = rows_cols(w)
        return remote(fs.at[w], db.at[x, c], fd_s.at[w], d_r.at[x, c], (2 * col + l, row))

    def mirror_copy(w):
        row, col = rows_cols(w)
        return remote(fm.at[w], mb.at[2 * l + c, x % 2], fm_s.at[w], m_r.at[2 * l + c, x % 2], (2 * row + x // 2, col))

    col_own = pair // 2
    dy = (col_own % 4 - y + 4) % 4
    dh = jnp.where(col_own // 4 != h, 1, 0)
    has_d = dy <= 2
    has_m = (dy >= 2) | ((dy == 0) & (dh == 1))
    d_here = (dh == 0) | (dy == 0)
    d_plane = jnp.where(d_here, g, other)
    m_plane = jnp.where(dy == 3, h * 4 + y_dn, jnp.where(dy == 2, h * 4 + y_far, other))
    local = (c == l) & d_here & has_d

    for j in range(4):
        load_copy(j).start()
    for i in range(4):
        small_copy(i).start()

    barrier = pltpu.get_barrier_semaphore()

    def greet(dev):
        pl.semaphore_signal(barrier, inc=1, device_id=dev, device_id_type=MESH)

    greet((pair, h * 4 + y_dn))
    greet((pair, h * 4 + y_up))
    greet((pair, other))
    greet((x * 4 + l * 2 + 1 - c, g))
    greet((x * 4 + (1 - l) * 2 + c, g))
    for d in (1, 2, 3):
        greet((((x + d) % 4) * 4 + l * 2 + c, g))
    for i in range(4):
        for cc in range(2):
            @pl.when(has_d & jnp.logical_not(local & (x == i) & (c == cc)))
            def _(i=i, cc=cc):
                greet((i * 4 + c * 2 + cc, d_plane))

            @pl.when(has_m)
            def _(i=i, cc=cc):
                greet(((2 * c + cc) * 4 + i, m_plane))
    expect = 8 + 11
    for w in range(4):
        expect = expect - jnp.where(stays(w), 1, 0)
    with scope("barrier"):
        pl.semaphore_wait(barrier, expect)

    with scope("first_sends"):
        for j in range(4):
            load_copy(j).wait()
            y1_copy(j).start()
            p_copy(j).start()
            if j < 2:
                tr_copy(j).start()

    with scope("weights"):
        for i in range(4):
            small_copy(i).wait()
        level = lax.broadcasted_iota(jnp.int32, (128, 128), 0)
        tv = jnp.broadcast_to(ve[...], (128, 128)).T
        tc0 = jnp.broadcast_to(ce[0:1, :], (128, 128)).T
        tc1 = jnp.broadcast_to(ce[1:2, :], (128, 128)).T
        for k in range(12):
            v_row = vb[k:k + 1, :]
            c_row = cb[k:k + 1, :]
            val = jnp.sum(jnp.where(level == v_row, tv, 0.0), axis=0, keepdims=True)
            con = jnp.sum(
                jnp.where(level == c_row, tc0, 0.0) + jnp.where(level + 128 == c_row, tc1, 0.0),
                axis=0, keepdims=True,
            )
            wt[k:k + 1, :] = 4.0 / ((val - con) * math.sqrt(pairs_total))

    def scale_into(src, j, dst):
        for k in range(12):
            tile = src[j, k // 6, (k % 6) * 128:(k % 6) * 128 + 128, :].astype(F32).T
            tile = (tile * wt[k:k + 1, :]).astype(BF16)
            rows = pl.ds(j * 128 if isinstance(j, int) else pl.multiple_of(j * 128, 128), 128)
            dst[k // 6, rows, (k % 6) * 128:(k % 6) * 128 + 128] = tile

    def dot(a, b):
        return lax.dot_general(a, b, (((1,), (0,)), ((), ())), preferred_element_type=F32)

    def csend(w, j, first=0, n=4, part=0):
        @pl.when(c != j % 2)
        def _():
            core_copy(w, j, first, n, part).start()

    def consume(w, j, first=0, n=4, part=0):
        jl = j // 2

        @pl.when(c == j % 2)
        def _():
            core_copy(w, j, first, n, part).wait_recv()
            for i in range(first, first + n):
                rows = pl.ds(i * 128, 128)

                @pl.when(x == i)
                def _():
                    xo[w, jl] = pp[w, j, rows, :] + cr[w, jl, rows, :]

                @pl.when(x != i)
                def _():
                    total = pp[w, j, rows, :] + cr[w, jl, rows, :]
                    if w == 0:
                        xs0[jl, i] = total
                    else:
                        xs[w - 1, jl, i] = total.astype(BF16)
                    x_copy(w, jl, i, x).start()

    def x_reduce(w, jl):
        for d in (1, 2, 3):
            x_copy(w, jl, 0, (x + d) % 4).wait_recv()
        total = xo[w, jl]
        for d in (1, 2, 3):
            if w == 0:
                total = total + xr0[jl, (x + d) % 4]
            else:
                total = total + xr[w - 1, jl, (x + d) % 4].astype(F32)
        tl[w, jl] = total

        @pl.when(l != jl)
        def _():
            l_copy(w).start()

    def deliver(w, jl):
        @pl.when(l == jl)
        def _():
            l_copy(w).wait_recv()
            total = tl[w, jl] + lr[w]
            fs[w] = total
            if w >= 1:
                fm[w] = total.T
                mirror_copy(w).start()
            if w >= 4:
                direct_copy(w).start()
            else:
                @pl.when(stays(w))
                def _():
                    db[x, c] = total

                @pl.when(jnp.logical_not(stays(w)))
                def _():
                    direct_copy(w).start()

    def forward(j):
        with scope("wait_tr"):
            tr_copy(j).wait_recv()
        y2_copy(j).start()
        if j < 2:
            tr_copy(j + 2).start()

    with scope("scale_own"):
        @pl.loop(0, 4)
        def _(j):
            scale_into(own, j, lo)

    with scope("mm_w0"):
        @pl.loop(0, 4)
        def _(j):
            pp[0, j] = dot(lo[0], own[j, 0]) + dot(lo[1], own[j, 1])
            csend(0, j)

    with scope("cons_w0"):
        @pl.loop(0, 4)
        def _(j):
            consume(0, j)

    forward(0)
    forward(1)

    def shell(w, k):
        right = (lambda j: dot(lp[kh, rows, :], y2b[j])) if w == 5 else (
            lambda j: dot(lp[0, rows, :], y1b[j, 0]) + dot(lp[1, rows, :], y1b[j, 1])
        )
        rows = pl.ds(0, 128 * (k + 1))
        pp[w, k, rows, :] = right(k)
        csend(w, k, 0, k + 1, 0)
        rows = pl.ds(128 * k, 128)
        for j in range(k):
            pp[w, j, rows, :] = right(j)
            csend(w, j, k, 1, k - j)

    def consume_shell(w, k):
        consume(w, k, 0, k + 1, 0)
        for j in range(k):
            consume(w, j, k, 1, k - j)

    for k in range(4):
        with scope("wait_y1"):
            y1_copy(k).wait_recv()
        with scope("mm_w1"):
            pp[1, k] = dot(lo[0], y1b[k, 0]) + dot(lo[1], y1b[k, 1])
            csend(1, k)
        if k in (1, 2):
            forward(k + 1)
        if k == 2:
            for w in (1, 3, 2):
                with scope("xred_early"):
                    x_reduce(w, 0)
        with scope("wait_p"):
            p_copy(k).wait_recv()
        with scope("mm_w3"):
            pp[3, k] = dot(lo[h], pb[k, h])
            csend(3, k)
        with scope("scale_p"):
            scale_into(pb, k, lp)
        with scope("cons1"):
            consume(1, k)
        with scope("mm_w4"):
            shell(4, k)
        with scope("cons3"):
            consume(3, k)
        with scope("wait_y2"):
            y2_copy(k).wait_recv()
        with scope("mm_w2"):
            pp[2, k] = dot(lo[kh], y2b[k])
            csend(2, k)
        with scope("cons4"):
            consume_shell(4, k)
        with scope("mm_w5"):
            shell(5, k)
        with scope("cons2"):
            consume(2, k)
        if k == 0:
            with scope("xred0"):
                x_reduce(0, 0)
                x_reduce(0, 1)
        if k == 1:
            with scope("deliver0"):
                deliver(0, 0)
                deliver(0, 1)
        if k == 2:
            with scope("del_early"):
                for w in (1, 3, 2):
                    deliver(w, 0)
        with scope("cons5"):
            consume_shell(5, k)

    for w in (1, 3, 4, 2, 5):
        for jl in range(2):
            if w >= 4 or jl == 1:
                with scope(f"xred_w{w}"):
                    x_reduce(w, jl)
    for w in (1, 3, 4, 2, 5):
        for jl in range(2):
            if w >= 4 or jl == 1:
                with scope(f"deliver_w{w}"):
                    deliver(w, jl)

    with scope("wait_final"):
        for i in range(4):
            for cc in range(2):
                @pl.when(has_d & jnp.logical_not(local & (x == i) & (c == cc)))
                def _(i=i, cc=cc):
                    remote(fs.at[0], db.at[i, cc], fd_s.at[0], d_r.at[i, cc], (pair, other)).wait_recv()

                @pl.when(has_m)
                def _(i=i, cc=cc):
                    remote(fm.at[1], mb.at[i, cc], fm_s.at[1], m_r.at[i, cc], (pair, other)).wait_recv()

    def emit(pick):
        for i in range(4):
            for cc in range(2):
                out[i * 128:(i + 1) * 128, cc * 128:(cc + 1) * 128] = pick(i, cc)

    with scope("emit"):
        @pl.when(has_d & has_m)
        def _():
            emit(lambda i, cc: db[i, cc] + mb[i, cc])

        @pl.when(has_d & jnp.logical_not(has_m))
        def _():
            emit(lambda i, cc: db[i, cc])

        @pl.when(jnp.logical_not(has_d))
        def _():
            emit(lambda i, cc: mb[i, cc])

    with scope("wait_sends"):
        for j in range(4):
            y1_copy(j).wait_send()
            p_copy(j).wait_send()
            tr_copy(j).wait_send()
            y2_copy(j).wait_send()

            @pl.when(c != j % 2)
            def _(j=j):
                for w in range(4):
                    core_copy(w, j, 0, 4, 0).wait_send()
                for w in (4, 5):
                    core_copy(w, j, 0, j + 1, 0).wait_send()
                    for k in range(j + 1, 4):
                        core_copy(w, j, k, 1, k - j).wait_send()

        for w in range(NB):
            for jl in range(2):
                for d in (1, 2, 3):
                    x_copy(w, jl, (x + d) % 4, x).wait_send()
            l_copy(w).wait_send()
            if w >= 1:
                mirror_copy(w).wait_send()
            if w >= 4:
                direct_copy(w).wait_send()
            else:
                @pl.when(jnp.logical_not(stays(w)))
                def _(w=w):
                    direct_copy(w).wait_send()


def per_device(densities, val_band, cond_band, val_energy, cond_energy):
    pairs, cols = densities.shape
    pairs_total = pairs * lax.axis_size("pair")
    vm = pltpu.VMEM
    dma = pltpu.SemaphoreType.DMA
    scratch = [
        vm((4, 2, 768, 128), BF16), vm((4, 2, 768, 128), BF16), vm((4, 768, 128), BF16),
        vm((4, 768, 128), BF16), vm((4, 2, 768, 128), BF16),
        vm((2, 512, 768), BF16), vm((2, 512, 768), BF16), vm((12, 128), F32),
        vm((12, 128), jnp.int32), vm((12, 128), jnp.int32), vm((1, 128), F32), vm((2, 128), F32),
        vm((NB, 4, 512, 128), F32), vm((NB, 2, 512, 128), F32),
        vm((2, 4, 128, 128), F32), vm((2, 4, 128, 128), F32),
        vm((NB - 1, 2, 4, 128, 128), BF16), vm((NB - 1, 2, 4, 128, 128), BF16),
        vm((NB, 2, 128, 128), F32), vm((NB, 2, 128, 128), F32), vm((NB, 128, 128), F32),
        vm((NB, 128, 128), F32), vm((NB, 128, 128), F32),
        vm((4, 2, 128, 128), F32), vm((4, 2, 128, 128), F32),
        dma((4,)), dma((4,)), dma((4,)), dma((4,)), dma((4,)), dma((4,)), dma((4,)), dma((4,)), dma((4,)), dma((4,)),
        dma((NB, 2, 4)), dma((NB, 2, 4)), dma((NB, 2, 4)), dma((NB, 2, 4)), dma((NB,)), dma((NB,)),
        dma((NB,)), dma((NB,)), dma((4, 2)), dma((4, 2)),
    ]
    in_vmem = pl.BlockSpec(memory_space=pltpu.VMEM)

    def body(*refs):
        kernel(pairs_total, *refs)

    return pl.pallas_call(
        body,
        name="chi",
        out_shape=jax.ShapeDtypeStruct((512, 256), F32),
        in_specs=[pl.BlockSpec(memory_space=pl.ANY)] * 5,
        out_specs=in_vmem,
        scratch_shapes=scratch,
        compiler_params=pltpu.CompilerParams(
            collective_id=0, has_side_effects=True, vmem_limit_bytes=62 * 1024 * 1024
        ),
    )(
        densities.reshape(2, pairs // 2, cols),
        val_band.reshape(12, 128),
        cond_band.reshape(12, 128),
        val_energy.reshape(1, 128),
        cond_energy.reshape(2, 128),
    )


def solution(mesh):
    placed = (P("pair", "ga"), P("pair"), P("pair"), P(), P())
    return jax.shard_map(
        per_device, mesh=mesh, in_specs=placed, out_specs=P("ga", "pair"), check_vma=False
    )
```

time: 290 us -> 87.5 us (0.30); the launches traced: 287 us -> 87.4 us
  waiting for transfers between devices: 260 us -> 0 us
  Pallas kernels: 0 us -> 85.5 us
  between operations: 13.4 us -> 0.01 us
  matrix products: 12 us -> 0 us
    all_gather x1 -> x0, waiting for transfers between devices: 160 us -> none  [per_device(): gathered = lax.all_gather(densities, 'ga', axis=1, tiled=True)]
    reduce_scatter x1 -> x0, waiting for transfers between devices: 98.6 us -> none  [per_device(): lax.psum_scatter(lax.dot_general(gathered, scaled, (((0,), (0,)), ((), ()...]
    pallas_call x0 -> x1, Pallas kernels: none -> 85.5 us  [per_device(): pl.pallas_call(body, name='chi', out_shape=jax.ShapeDtypeStruct((512, 256...]
    dot_general x1 -> x0, matrix products: 12 us -> none  [per_device(): lax.dot_general(gathered, scaled, (((0,), (0,)), ((), ())), preferred_ele...]
  transfers between devices with their start and end apart: 2 -> 0, of which waited for: 2 -> 0; matrix products, arithmetic and copies ran while one was open for 1% -> 0% of each run, Pallas kernels for 0% -> 0%
where the time goes in v2:
time: 87.5 us; the launch traced here: 87.4 us
  Pallas kernels  85.5 us (98%)
  local copies, waits for them, and re-layouts  1.87 us (2%)
    pallas_call x1, Pallas kernels, per_device(): pl.pallas_call(body, name='chi', out_shape=jax.ShapeDtypeStruct((512, 256...  85.5 us
    unnamed x1, local copies, waits for them, and re-layouts  1.87 us

profile of v2, /device:TPU:67, one launch (start us, length us, event | category | flops | bytes accessed | tf_op | source)
XLA Modules:
  0.0 87.4 jit_solution(4858665878165481998)
XLA Ops:
  0.0 85.5 %chi.1 = f32[512,256]{1,0:T(8,128)} custom-call(bf16[2,768,512]{2,1,0:T(8,128)(2,1)} %bitcast.5, s32[12,128]{1,0:T(8,128)} %bitcast.6, s32[12,128]{1,0:T(8,128)} %bitcast.7, f32[1,128]{1,0:T(1,128)} %bitcast.9, f32[2,128]{1,0:T(2,128)} %bitcast.8), custom_call_target="tpu_custom_call" | custom-call | tf_op jit(solution)/shard_map/chi/pallas_call | solution.py:422
  85.5 1.9 %copy.7 = f32[512,256]{1,0:T(8,128)} copy(f32[512,256]{1,0:T(8,128)} %chi.1) | data formatting | bytes 1048576
